TPU v7x, 32 devices: a whole 2x2x4 slice. The times are simulated.
32 devices in a mesh: node: 4 (over y, x), torus: 8 (over z, core).
Axes of the slice: x: 2, y: 2, z: 4, core: 2. Of those that a mesh axis runs over, the one named last changes fastest.
Arguments:
- tokens: bfloat16 [4096, 7168], P(('node', 'torus')), may hold values from -6 to 6
- expert_ids: int32 [4096, 8], P(('node', 'torus')), may hold values from 0 to 383, as said below
- route_weight: bfloat16 [4096, 8], P(('node', 'torus')), may hold values from 0.19921875 to 2.5
- w_gate: bfloat16 [16, 7168, 1024], P('torus', None, 'node'), may hold values from -0.0625 to 0.0625
- w_up: bfloat16 [16, 7168, 1024], P('torus', None, 'node'), may hold values from -0.0625 to 0.0625
- w_down: bfloat16 [16, 1024, 7168], P('torus', 'node'), may hold values from -0.1875 to 0.1875
Outputs:
- moe_out: bfloat16 [4096, 7168], P(('node', 'torus'))
Inputs may be any that keep to these rules, and one draw needn't show every extreme that they name: `expert_ids`: each row names 8 different experts. Counting an expert e below 16 as one of group e // 2, at most 4 of the 128 rows of one device (aligned blocks of rows, in order) name an expert of any one group, and in every draw some group is named by exactly 4 rows of every device.
All inputs are finite; a program needn't handle non-finite values.
Results may differ from a plain program's by a relative error of at most 0.0095.
Values may be sent and summed in bfloat16 or wider, within the bound.
A program may use at most 128 MiB of HBM per device.

v0:
```python
import jax
import jax.numpy as jnp
from jax import lax
from jax.sharding import PartitionSpec as P

EXP_DEV = 2
CAP = 4
QBLOCK = 128


def quantize(tokens):
    count = tokens.shape[0]
    blocks = tokens.astype(jnp.float32).reshape(count, -1, QBLOCK)
    largest = jnp.max(jnp.abs(blocks), axis=-1)
    scale = ((largest + 1e-06) * (1.0 / 448.0)).astype(jnp.bfloat16)
    scale = lax.optimization_barrier(scale)
    quantized = (blocks / scale.astype(jnp.float32)[:, :, None]).astype(jnp.bfloat16)
    quantized = lax.optimization_barrier(quantized)
    return (quantized.reshape(count, -1), scale)


def restore(quantized, scale):
    count = quantized.shape[0]
    blocks = (
        quantized.astype(jnp.float32).reshape(count, -1, QBLOCK)
        * scale.astype(jnp.float32)[:, :, None]
    )
    return blocks.astype(jnp.bfloat16).reshape(count, -1)


def shards(tokens, expert_ids, route_weight, w_gate, w_up, w_down):
    nodes = lax.axis_size("node")
    groups = lax.axis_size("torus")
    local_rows = tokens.shape[0]
    width = tokens.shape[1]
    window = EXP_DEV * groups
    quantized, scale = quantize(tokens)
    experts = jnp.arange(window, dtype=jnp.int32)
    matched = expert_ids[:, :, None] == experts[None, None, :]
    route_sel = jnp.sum(
        jnp.where(matched, route_weight.astype(jnp.float32)[:, :, None], jnp.float32(0.0)), axis=1
    )
    member = (
        jnp.any(matched, axis=1).reshape(local_rows, groups, EXP_DEV).any(axis=-1).astype(jnp.int32)
    )
    slot_index = jnp.cumsum(member, axis=0) - member
    capacity_ids = jnp.arange(CAP, dtype=jnp.int32)
    placing = (member.T[:, None, :] == 1) & (
        slot_index.T[:, None, :] == capacity_ids[None, :, None]
    )
    placing = placing.astype(jnp.bfloat16)
    send_rows = jnp.einsum(
        "gcr,rd->gcd", placing, quantized, preferred_element_type=jnp.float32
    ).astype(jnp.bfloat16)
    send_scale = jnp.einsum(
        "gcr,rb->gcb", placing, scale, preferred_element_type=jnp.float32
    ).astype(jnp.bfloat16)
    route_three = route_sel.reshape(local_rows, groups, EXP_DEV).astype(jnp.bfloat16)
    send_weights = jnp.einsum(
        "gcr,rgj->gcj", placing, route_three, preferred_element_type=jnp.float32
    ).astype(jnp.bfloat16)
    arrived_rows = lax.all_gather(
        lax.all_to_all(send_rows, "torus", split_axis=0, concat_axis=0, tiled=True),
        "node",
        axis=0,
        tiled=True,
    )
    senders = arrived_rows.shape[0]
    slots = arrived_rows.shape[1]
    flat_rows = senders * slots
    restored = restore(
        arrived_rows.reshape(flat_rows, width),
        lax.all_gather(
            lax.all_to_all(send_scale, "torus", split_axis=0, concat_axis=0, tiled=True),
            "node",
            axis=0,
            tiled=True,
        ).reshape(flat_rows, -1),
    )
    weights = (
        lax.all_gather(
            lax.all_to_all(send_weights, "torus", split_axis=0, concat_axis=0, tiled=True),
            "node",
            axis=0,
            tiled=True,
        )
        .reshape(flat_rows, EXP_DEV)
        .astype(jnp.float32)
    )
    partial_value = jnp.zeros((flat_rows, width), jnp.float32)
    for expert in range(EXP_DEV):
        gate = jnp.dot(restored, w_gate[expert], preferred_element_type=jnp.float32)
        upper = jnp.dot(restored, w_up[expert], preferred_element_type=jnp.float32)
        hidden = (jax.nn.silu(gate) * upper).astype(jnp.bfloat16)
        result = jnp.dot(hidden, w_down[expert], preferred_element_type=jnp.float32)
        partial_value = partial_value + weights[:, expert : expert + 1] * result
    partial_value = partial_value.reshape(senders, slots, width)
    slots = partial_value.shape[1]
    returned = lax.all_to_all(
        partial_value.astype(jnp.bfloat16),
        ("node", "torus"),
        split_axis=0,
        concat_axis=0,
        tiled=True,
    )
    summed = returned.astype(jnp.float32).reshape(nodes, groups, slots, width).sum(axis=0)
    combined = summed.astype(jnp.bfloat16)
    output = jnp.einsum("gcr,gcd->rd", placing, combined, preferred_element_type=jnp.float32)
    return output.astype(jnp.bfloat16)


def solution(mesh):
    placed = (
        P(("node", "torus"), None),
        P(("node", "torus"), None),
        P(("node", "torus"), None),
        P("torus", None, "node"),
        P("torus", None, "node"),
        P("torus", "node", None),
    )
    return jax.shard_map(
        shards, mesh=mesh, in_specs=placed, out_specs=P(("node", "torus"), None), check_vma=False
    )
```

profile of v0, /device:TPU:0, one launch (start us, length us, event | category | flops | bytes accessed | tf_op | source)
XLA Modules:
  0.0 157.3 jit_solution(290229022102486248)
XLA Ops:
  6.5 0.7 fusion.68
  7.3 0.1 copy.53
  7.5 0.2 reduce_window_sum.11
  7.7 1.9 %convert_bitcast_fusion = f32[16,8,56,128]{3,1,2,0:T(8,128)S(1)} fusion(bf16[128,7168]{1,0:T(8,128)(2,1)} %param.6), kind=kLoop, calls=%fused_computation.17 | loop fusion | flops 917504 | bytes 5505024
  9.6 0.6 copy.65
  10.3 1.0 abs_reduce_fusion
  11.3 2.3 %divide_convert_fusion = bf16[128,56,128]{2,1,0:T(8,128)(2,1)} fusion(f32[128,56]{1,0:T(8,128)S(1)} %convert_element_type.130, f32[16,8,56,128]{3,2,1,0:T(8,128)S(1)} %copy.65), kind=kLoop, calls=%fused_computation.25 | loop fusion | flops 1835008 | bytes 5533696 | tf_op jit(solution)/shard_map/convert_element_type | solution.py:17
  13.6 2.7 %reshape.96 = bf16[128,7168,1]{1,0,2:T(8,128)(2,1)S(1)} reshape(bf16[128,56,128]{2,1,0:T(8,128)(2,1)} %divide_convert_fusion) | data formatting | bytes 3670016 | tf_op jit(solution)/shard_map/reshape | solution.py:19
  16.4 0.4 convolution_convert_fusion
  16.8 0.4 copy.59
  17.1 20.2 %all_to_all.20 = bf16[8,4,7168]{2,1,0:T(4,128)(2,1)} all-to-all(bf16[8,4,7168]{2,1,0:T(4,128)(2,1)S(1)} %copy.59), channel_id=1, replica_groups=mesh['node'=4,'torus'=8] {'torus'}, dimensions={0} | all-to-all | bytes 917504 | tf_op jit(solution)/shard_map/all_to_all | solution.py:63
  37.4 0.7 convolution_convert_fusion.2
  38.1 3.3 %all-to-all-start = ((bf16[8,4,2]{1,2,0:T(2,128)(2,1)}), bf16[8,4,2]{1,2,0:T(2,128)(2,1)S(1)}, u32[]{:S(2)}, u32[]{:S(2)}) async-start(bf16[8,4,2]{1,2,0:T(2,128)(2,1)} %convolution_convert_fusion.2), calls=%async_computation | async-start | bytes 8192 | tf_op jit(solution)/shard_map/all_to_all | solution.py:82
  41.4 0.1 convolution_convert_fusion.1
  41.5 0.6 copy.61
  42.2 4.8 %all-to-all-done = bf16[8,4,2]{1,2,0:T(2,128)(2,1)S(1)} async-done(((bf16[8,4,2]{1,2,0:T(2,128)(2,1)}), bf16[8,4,2]{1,2,0:T(2,128)(2,1)S(1)}, u32[]{:S(2)}, u32[]{:S(2)}) %all-to-all-start) | async-done | bytes 160 | tf_op jit(solution)/shard_map/all_to_all | solution.py:82
  46.9 3.3 %all-to-all-start.2 = ((bf16[8,4,56]{2,1,0:T(4,128)(2,1)}), bf16[8,4,56]{2,1,0:T(4,128)(2,1)S(1)}, u32[]{:S(2)}, u32[]{:S(2)}) async-start(bf16[8,4,56]{2,1,0:T(4,128)(2,1)} %copy.61), calls=%async_computation.2 | async-start | bytes 16384 | tf_op jit(solution)/shard_map/all_to_all | solution.py:74
  50.3 8.2 %all_gather.9 = bf16[32,4,2]{1,2,0:T(2,128)(2,1)S(1)} all-gather(bf16[8,4,2]{1,2,0:T(2,128)(2,1)S(1)} %all-to-all-done), channel_id=1, replica_groups=mesh['node'=4,'torus'=8] {'node'}, dimensions={0}, use_global_device_ids=true | all-gather | bytes 640 | tf_op jit(solution)/shard_map/all_gather | solution.py:81
  58.6 0.1 copy.58
  58.7 0.1 reshape.91
  58.8 8.8 %all_gather.11 = bf16[32,4,56]{2,1,0:T(4,128)(2,1)S(1)} all-gather(bf16[8,4,56]{2,1,0:T(4,128)(2,1)S(1)} %all-to-all-done.2), channel_id=1, replica_groups=mesh['node'=4,'torus'=8] {'node'}, dimensions={0}, use_global_device_ids=true | all-gather | bytes 17920 | tf_op jit(solution)/shard_map/all_gather | solution.py:73
  67.6 2.2 %all-gather.2.cloned.1.call-done = bf16[32,4,7168]{2,1,0:T(4,128)(2,1)} async-done(((bf16[8,4,7168]{2,1,0:T(4,128)(2,1)}), bf16[32,4,7168]{2,1,0:T(4,128)(2,1)}) %all-gather.2.cloned.1.call-update) | async-done | bytes 1835024 | tf_op jit(solution)/shard_map/all_gather | solution.py:62
  69.8 4.3 %reshape.94 = f32[128,56,128]{2,1,0:T(8,128)} reshape(bf16[32,4,7168]{2,1,0:T(4,128)(2,1)} %all-gather.2.cloned.1.call-done) | data formatting | bytes 5505024 | tf_op jit(solution)/shard_map/convert_element_type | solution.py:25
  74.1 2.6 %multiply_convert_fusion = bf16[128,56,128]{2,1,0:T(8,128)(2,1)S(1)} fusion(f32[128,56,128]{2,1,0:T(8,128)} %reshape.94, f32[128,56]{1,0:T(8,128)S(1)} %convert.6), kind=kLoop, calls=%fused_computation.24 | loop fusion | flops 1835008 | bytes 5533696 | tf_op jit(solution)/shard_map/convert_element_type | solution.py:28
  76.7 3.3 %fusion.6 = f32[128,256]{1,0:T(8,128)S(1)} fusion(bf16[2,7168,256]{2,1,0:T(8,128)(2,1)} %param.9, bf16[16,8,56,128]{3,2,1,0:T(8,128)(2,1)S(1)} %bitcast.86), kind=kOutput, calls=%fused_computation.10 | convolution fusion | flops 469762048 | bytes 5636096 | tf_op jit(solution)/shard_map/dot_general | solution.py:92
  80.1 2.7 %fusion.11 = f32[128,256]{1,0:T(8,128)S(1)} fusion(bf16[2,7168,256]{2,1,0:T(8,128)(2,1)} %param.9, bf16[16,8,56,128]{3,2,1,0:T(8,128)(2,1)S(1)} %bitcast.87), kind=kOutput, calls=%fused_computation.15 | convolution fusion | flops 469762048 | bytes 5636096 | tf_op jit(solution)/shard_map/dot_general | solution.py:92
  82.8 7.1 %convolution_multiply_fusion.1 = f32[128,7168]{1,0:T(8,128)} fusion(bf16[2,256,7168]{2,1,0:T(8,128)(2,1)} %param.11, f32[128]{0:T(128)S(1)} %get-tuple-element.8, bf16[2,7168,256]{2,1,0:T(8,128)(2,1)} %param.10, bf16[16,8,56,128]{3,2,1,0:T(8,128)(2,1)S(1)} %bitcast.88, f32[128,256]{1,0:T(8,128)S(1)} %fusion.11), kind=kOutput, calls=%fused_computation.3 | convolution fusion | flops 940638208 | bytes 12976640 | tf_op jit(solution)/shard_map/dot_general | solution.py:95
  89.9 6.9 %fusion.1 = bf16[128,7168]{1,0:T(8,128)(2,1)S(1)} fusion(f32[128,7168]{1,0:T(8,128)} %convolution_multiply_fusion.1, bf16[2,256,7168]{2,1,0:T(8,128)(2,1)} %param.11, f32[128]{0:T(128)S(1)} %get-tuple-element.7, bf16[2,7168,256]{2,1,0:T(8,128)(2,1)} %param.10, bf16[16,8,56,128]{3,2,1,0:T(8,128)(2,1)} %bitcast.89, f32[128,256]{1,0:T(8,128)S(1)} %fusion.6), kind=kOutput, calls=%fused_computation.4 | convolution fusion | flops 942473216 | bytes 14811648 | tf_op jit(solution)/shard_map/dot_general | solution.py:95
  96.8 1.6 %convert_element_type.143 = bf16[32,4,7168]{2,1,0:T(4,128)(2,1)} reshape(bf16[128,7168]{1,0:T(8,128)(2,1)S(1)} %fusion.1) | data formatting | bytes 3670016 | tf_op jit(solution)/shard_map/convert_element_type | solution.py:100
  98.4 48.9 %all_to_all.21 = bf16[32,4,7168]{2,1,0:T(4,128)(2,1)S(1)} all-to-all(bf16[32,4,7168]{2,1,0:T(4,128)(2,1)} %convert_element_type.143), channel_id=1, replica_groups=mesh['node'=4,'torus'=8] {'node','torus'}, dimensions={0} | all-to-all | bytes 3670016 | tf_op jit(solution)/shard_map/all_to_all | solution.py:99
  147.2 1.3 reduce
  148.5 1.9 %fusion.2 = bf16[128,7168]{1,0:T(8,128)(2,1)} fusion(pred[8,4,128]{2,0,1:T(8,128)(4,1)S(1)} %fusion.70, bf16[8,4,7168]{2,1,0:T(4,128)(2,1)S(1)} %reduce), kind=kOutput, calls=%fused_computation.5 | convolution fusion | flops 59637760 | bytes 2297856 | tf_op jit(solution)/shard_map/gcr,gcd->rd/dot_general | solution.py:108
  (23 shorter events, 0.4 us)
Async XLA Ops:
  6.5 63.2 %all-gather.2.cloned.1.call-start = ((), (), s32[]{:S(2)}) async-start(), calls=%async_computation.4 | async-start | bytes 2293760 | tf_op jit(solution)/shard_map/all_gather | solution.py:62
  13.6 23.7 %copy-start.2 = (bf16[128,8]{0,1:T(8,128)(2,1)S(1)}, bf16[128,8]{0,1:T(8,128)(2,1)}, u32[]{:S(2)}) copy-start(bf16[128,8]{0,1:T(8,128)(2,1)} %param.8) | copy-start | bytes 6148
  13.6 23.7 %copy-start.1 = (s32[128,8]{0,1:T(8,128)S(1)}, s32[128,8]{0,1:T(8,128)}, u32[]{:S(2)}) copy-start(s32[128,8]{0,1:T(8,128)} %param.7) | copy-start | bytes 12292
  38.1 8.8 %all-to-all-start = ((bf16[8,4,2]{1,2,0:T(2,128)(2,1)}), bf16[8,4,2]{1,2,0:T(2,128)(2,1)S(1)}, u32[]{:S(2)}, u32[]{:S(2)}) async-start(bf16[8,4,2]{1,2,0:T(2,128)(2,1)} %convolution_convert_fusion.2), calls=%async_computation | async-start | bytes 8192 | tf_op jit(solution)/shard_map/all_to_all | solution.py:82
  46.9 11.9 %all-to-all-start.2 = ((bf16[8,4,56]{2,1,0:T(4,128)(2,1)}), bf16[8,4,56]{2,1,0:T(4,128)(2,1)S(1)}, u32[]{:S(2)}, u32[]{:S(2)}) async-start(bf16[8,4,56]{2,1,0:T(4,128)(2,1)} %copy.61), calls=%async_computation.2 | async-start | bytes 16384 | tf_op jit(solution)/shard_map/all_to_all | solution.py:74
  76.7 6.1 %copy-start = (bf16[128,56,128]{2,1,0:T(8,128)(2,1)}, bf16[128,56,128]{2,1,0:T(8,128)(2,1)S(1)}, u32[]{:S(2)}) copy-start(bf16[128,56,128]{2,1,0:T(8,128)(2,1)S(1)} %multiply_convert_fusion) | copy-start | bytes 5505028
Sparse Core Ops, SparseCore 0:
  37.5 32.2 all-gather.1
where the time goes:
time: 158 us; the launch traced here: 157 us
  blocking collectives  86 us (54%)
  matrix products  23.1 us (15%)
  between operations  13.6 us (9%)
  local copies, waits for them, and re-layouts  10.9 us (7%)
  other arithmetic  10.1 us (6%)
  waiting for transfers between devices  6.97 us (4%)
  starting transfers between devices  6.65 us (4%)
    all_to_all x1, blocking collectives, shards(): lax.all_to_all(partial_value.astype(jnp.bfloat16), ('node', 'torus'), spl...  48.9 us
    all_to_all x1, blocking collectives, shards(): lax.all_to_all(send_rows, 'torus', split_axis=0, concat_axis=0, tiled=True)  20.2 us
    dot_general x2, matrix products, shards(): result = jnp.dot(hidden, w_down[expert], preferred_element_type=jnp.float32)  14 us
    all_gather x1, blocking collectives, shards(): lax.all_gather(lax.all_to_all(send_scale, 'torus', split_axis=0, concat_a...  8.75 us
    all_gather x1, blocking collectives, shards(): lax.all_gather(lax.all_to_all(send_weights, 'torus', split_axis=0, concat...  8.19 us
    dot_general x2, matrix products, shards(): gate = jnp.dot(restored, w_gate[expert], preferred_element_type=jnp.float32)  6.03 us
    all_to_all x1, waiting for transfers between devices, shards(): lax.all_to_all(send_weights, 'torus', split_axis=0, concat_axis=0, tiled=...  4.78 us
    convert_element_type x1, local copies, waits for them, and re-layouts, restore(): quantized.astype(jnp.float32).reshape(count, -1, QBLOCK)  4.33 us
  transfers between devices with their start and end apart: 3, of which 2 were waited for; matrix products, arithmetic and copies ran while one was open for 1% of the time, Pallas kernels for 0%

commit v1 on v0

v1 whole, which is shorter than its diff:
```python
import functools

import jax
import jax.numpy as jnp
from jax import lax
from jax.experimental import pallas as pl
from jax.experimental.pallas import tpu as pltpu
from jax.sharding import PartitionSpec as P

CAP = 4
QBLOCK = 128
PARTS = 4
SUB = CAP * PARTS
CHUNK = 1024
WIDE = CHUNK // PARTS
MESH = pl.DeviceIdType.MESH
F32 = jnp.float32
BF16 = jnp.bfloat16


def flipped(index, mask):
    value = index
    bit = 0
    while mask >> bit:
        if (mask >> bit) & 1:
            size = 1 << bit
            value = value + size * (1 - 2 * lax.rem(lax.div(index, jnp.int32(size)), jnp.int32(2)))
        bit += 1
    return value


def dot(left, right):
    return jnp.dot(left, right, preferred_element_type=F32)


def kernel(
    groups, chunks, lags,
    tok_hbm, ids_ref, rw_ref, wg_hbm, wu_hbm, wd_hbm, out_hbm,
    tok, wg, wu, wd, place, place_t, perm, perm_t,
    sent, held, wsent, wheld, xs, acc, hidden, wcol,
    part, relay_a, relay_b, got_x, got_y, back_s, back, obuf,
    sems, lsems,
):
    node = lax.axis_index("node")
    torus = lax.axis_index("torus")
    rows = tok.shape[0]
    subs = groups * SUB
    slots = groups * CAP
    half = slots // 2
    shalf = subs // 2
    units = subs // 128
    experts = wg.shape[0]
    at_x = (flipped(node, 1), torus)
    at_y = (flipped(node, 2), torus)
    at_z = [(node, flipped(torus, j)) for j in range(groups)]

    tok_cp, wg_cp, wu_cp, wd_cp = [], [], [], []
    for k in range(chunks):
        cols = pl.ds(k * CHUNK, CHUNK)
        tok_cp.append(pltpu.make_async_copy(tok_hbm.at[:, cols], tok.at[:, cols], lsems.at[0, k]))
        wg_cp.append(pltpu.make_async_copy(wg_hbm.at[:, cols, :], wg.at[:, cols, :], lsems.at[1, k]))
        wu_cp.append(pltpu.make_async_copy(wu_hbm.at[:, cols, :], wu.at[:, cols, :], lsems.at[2, k]))
        wd_cp.append(pltpu.make_async_copy(wd_hbm.at[:, :, cols], wd.at[:, :, cols], lsems.at[3, k]))
    for c in tok_cp:
        c.start()
    for a, b in zip(wg_cp, wu_cp):
        a.start()
        b.start()
    for c in wd_cp:
        c.start()

    barrier = pltpu.get_barrier_semaphore()
    for peer in at_z[1:] + [at_x, at_y]:
        pl.semaphore_signal(barrier, inc=1, device_id=peer, device_id_type=MESH)

    col = lax.broadcasted_iota(jnp.int32, (rows, subs), 1)
    gid = jnp.bitwise_xor(col // SUB, jnp.full((rows, subs), torus, jnp.int32))
    slot_of = (col // PARTS) % CAP
    part_of = col % PARTS
    hit = jnp.zeros((rows, subs), F32)
    chosen = [jnp.zeros((rows, subs), F32) for _ in range(experts)]
    for k in range(ids_ref.shape[1]):
        named = jnp.broadcast_to(ids_ref[:, k : k + 1], (rows, subs))
        weight = jnp.broadcast_to(rw_ref[:, k : k + 1], (rows, subs))
        for e in range(experts):
            same = named == gid * experts + e
            hit = jnp.where(same, 1.0, hit)
            chosen[e] = jnp.where(same, weight, chosen[e])
    lower = lax.broadcasted_iota(jnp.int32, (rows, rows), 1) < lax.broadcasted_iota(
        jnp.int32, (rows, rows), 0
    )
    before = dot(lower.astype(F32).astype(BF16), hit.astype(BF16))
    onehot = jnp.where(before == slot_of.astype(F32), hit, 0.0)
    for q in range(PARTS):
        mine = jnp.where(part_of == q, onehot, 0.0)
        place_t[q] = mine.astype(BF16)
        place[q] = mine.T.astype(BF16)
    lane = lax.broadcasted_iota(jnp.int32, (subs, 128), 1)
    wrow = jnp.zeros((subs, 128), F32)
    for e in range(experts):
        total = jnp.sum((onehot * chosen[e]).T, axis=1, keepdims=True)
        wrow = jnp.where(lane == e, total, wrow)
    wsent[...] = wrow.astype(BF16)
    wheld[0, 0:SUB] = wrow[0:SUB].astype(BF16)
    pr = lax.broadcasted_iota(jnp.int32, (128, 128), 0)
    pc = lax.broadcasted_iota(jnp.int32, (128, 128), 1)
    ur = 128 // PARTS
    perm[...] = (pc == (pr % ur) * PARTS + pr // ur).astype(F32).astype(BF16)
    perm_t[...] = (pr == (pc % ur) * PARTS + pc // ur).astype(F32).astype(BF16)

    pl.semaphore_wait(barrier, groups + 1)

    def remote(src, dst, a, b, k, peer):
        copy = pltpu.make_async_remote_copy(
            src_ref=src, dst_ref=dst, send_sem=sems.at[a, k], recv_sem=sems.at[b, k],
            device_id=peer, device_id_type=MESH,
        )
        copy.start()

    def wait(ref, a, k):
        pltpu.make_async_copy(ref, ref, sems.at[a, k]).wait()

    def views(k):
        if k == chunks:
            return wsent, wheld
        return sent.at[k], held.at[k]

    def exchange(k):
        src, dst = views(k)
        for j in range(1, groups):
            at = pl.ds(j * SUB, SUB)
            remote(src.at[at], dst.at[0, at], 0, 1, k, at_z[j])

    def spread(k):
        _, dst = views(k)
        wait(dst.at[0, pl.ds(SUB, subs - SUB)], 1, k)
        remote(dst.at[0], dst.at[1], 2, 3, k, at_x)
        remote(dst.at[0], dst.at[2], 4, 5, k, at_y)

    def forward(k):
        _, dst = views(k)
        wait(dst.at[1], 3, k)
        remote(dst.at[1, pl.ds(0, shalf)], dst.at[3, pl.ds(0, shalf)], 6, 7, k, at_y)
        wait(dst.at[2], 5, k)
        remote(dst.at[2, pl.ds(shalf, shalf)], dst.at[3, pl.ds(shalf, shalf)], 8, 9, k, at_x)

    def arrived(k):
        _, dst = views(k)
        wait(dst.at[3, pl.ds(0, shalf)], 7, k)
        wait(dst.at[3, pl.ds(shalf, shalf)], 9, k)

    def make(k):
        tok_cp[k].wait()
        picked = jnp.zeros((subs, WIDE), F32)
        for q in range(PARTS):
            picked += dot(place[q], tok[:, k * CHUNK + q * WIDE : k * CHUNK + (q + 1) * WIDE])
        for b in range(WIDE // QBLOCK):
            block = picked[:, b * QBLOCK : (b + 1) * QBLOCK]
            largest = jnp.max(jnp.abs(block), axis=1, keepdims=True)
            scale = ((largest + 1e-06) * (1.0 / 448.0)).astype(BF16).astype(F32)
            coded = (block / scale).astype(BF16).astype(F32)
            value = (coded * scale).astype(BF16)
            sent[k, :, b * QBLOCK : (b + 1) * QBLOCK] = value
            held[k, 0, 0:SUB, b * QBLOCK : (b + 1) * QBLOCK] = value[0:SUB]

    def unit_rows(r, u):
        return r * slots + u * ur

    def multiply(k):
        for r in range(4):
            for u in range(units):
                moved = dot(perm[...], held[k, r, u * 128 : (u + 1) * 128, :]).astype(BF16)
                at = unit_rows(r, u)
                for q in range(PARTS):
                    xs[at : at + ur, q * WIDE : (q + 1) * WIDE] = moved[q * ur : (q + 1) * ur]
        wg_cp[k].wait()
        wu_cp[k].wait()
        cols = pl.ds(k * CHUNK, CHUNK)
        for e in range(experts):
            for s, w in enumerate((wg, wu)):
                got = dot(xs[...], w[e, cols, :])
                if k == 0:
                    acc[e, s] = got
                else:
                    acc[e, s] += got

    exchange(chunks)
    l2, l3, l4 = lags
    for step in range(chunks + l4):
        if step < chunks:
            make(step)
            exchange(step)
        if step == l2:
            spread(chunks)
        if 0 <= step - l2 < chunks:
            spread(step - l2)
        if step == l3:
            forward(chunks)
        if 0 <= step - l3 < chunks:
            forward(step - l3)
        if step == l4:
            arrived(chunks)
            for r in range(4):
                for u in range(units):
                    moved = dot(perm[...], wheld[r, u * 128 : (u + 1) * 128, :])
                    at = unit_rows(r, u)
                    wcol[at : at + ur, :] = moved[0:ur]
        if 0 <= step - l4 < chunks:
            arrived(step - l4)
            multiply(step - l4)

    for e in range(experts):
        gate = acc[e, 0]
        hidden[e] = (gate / (1.0 + jnp.exp(-gate)) * acc[e, 1]).astype(BF16)

    def down(k):
        wd_cp[k].wait()
        for r in range(4):
            at = pl.ds(r * slots, slots)
            total = jnp.zeros((slots, CHUNK), F32)
            for e in range(experts):
                got = dot(hidden[e, at, :], wd[e, :, k * CHUNK : (k + 1) * CHUNK])
                total += wcol[at, e : e + 1] * got
            part[k, r] = total.astype(BF16)
        remote(part.at[k, 3, pl.ds(0, half)], relay_a.at[k], 10, 11, k, at_y)
        remote(part.at[k, 3, pl.ds(half, half)], relay_b.at[k], 12, 13, k, at_x)

    def merge(k):
        wait(relay_a.at[k], 11, k)
        part[k, 1, 0:half] = (part[k, 1, 0:half].astype(F32) + relay_a[k].astype(F32)).astype(BF16)
        remote(part.at[k, 1], got_x.at[k], 14, 15, k, at_x)
        wait(relay_b.at[k], 13, k)
        part[k, 2, half:slots] = (
            part[k, 2, half:slots].astype(F32) + relay_b[k].astype(F32)
        ).astype(BF16)
        remote(part.at[k, 2], got_y.at[k], 16, 17, k, at_y)

    def home(k):
        wait(got_x.at[k], 15, k)
        wait(got_y.at[k], 17, k)
        for u in range(units):
            at = pl.ds(u * ur, ur)
            total = (
                part[k, 0, at].astype(F32) + got_x[k, at].astype(F32) + got_y[k, at].astype(F32)
            ).astype(BF16)
            stacked = jnp.concatenate(
                [total[:, q * WIDE : (q + 1) * WIDE] for q in range(PARTS)], axis=0
            )
            moved = dot(perm_t[...], stacked).astype(BF16)
            back_s[k, u * 128 : (u + 1) * 128] = moved
            if u == 0:
                back[k, 0:SUB] = moved[0:SUB]
        for j in range(1, groups):
            at = pl.ds(j * SUB, SUB)
            remote(back_s.at[k, at], back.at[k, at], 18, 19, k, at_z[j])

    out_cp = [
        pltpu.make_async_copy(obuf.at[k], out_hbm.at[:, pl.ds(k * CHUNK, CHUNK)], lsems.at[4, k])
        for k in range(chunks)
    ]

    def finish(k):
        wait(back.at[k, pl.ds(SUB, subs - SUB)], 19, k)
        for q in range(PARTS):
            obuf[k, :, q * WIDE : (q + 1) * WIDE] = dot(place_t[q], back[k]).astype(BF16)
        out_cp[k].start()

    for step in range(chunks + l4):
        if step < chunks:
            down(step)
        if 0 <= step - l2 < chunks:
            merge(step - l2)
        if 0 <= step - l3 < chunks:
            home(step - l3)
        if 0 <= step - l4 < chunks:
            finish(step - l4)

    for k in range(chunks + 1):
        src, dst = views(k)
        wait(src.at[pl.ds(SUB, subs - SUB)], 0, k)
        wait(dst.at[0], 2, k)
        wait(dst.at[0], 4, k)
        wait(dst.at[1, pl.ds(0, shalf)], 6, k)
        wait(dst.at[2, pl.ds(shalf, shalf)], 8, k)
    for k in range(chunks):
        wait(relay_a.at[k], 10, k)
        wait(relay_b.at[k], 12, k)
        wait(got_x.at[k], 14, k)
        wait(got_y.at[k], 16, k)
        wait(back_s.at[k, pl.ds(SUB, subs - SUB)], 18, k)
        out_cp[k].wait()


LAGS = (1, 2, 3)


def shards(tokens, expert_ids, route_weight, w_gate, w_up, w_down):
    groups = lax.axis_size("torus")
    rows, width = tokens.shape
    experts, _, units = w_gate.shape
    chunks = width // CHUNK
    subs = groups * SUB
    slots = groups * CAP
    anywhere = pl.BlockSpec(memory_space=pl.ANY)
    local = pl.BlockSpec(memory_space=pltpu.VMEM)
    V = pltpu.VMEM
    return pl.pallas_call(
        functools.partial(kernel, groups, chunks, LAGS),
        out_shape=jax.ShapeDtypeStruct((rows, width), BF16),
        in_specs=[anywhere, local, local, anywhere, anywhere, anywhere],
        out_specs=anywhere,
        scratch_shapes=[
            V((rows, width), BF16),
            V(w_gate.shape, BF16),
            V(w_up.shape, BF16),
            V(w_down.shape, BF16),
            V((PARTS, subs, rows), BF16),
            V((PARTS, rows, subs), BF16),
            V((128, 128), BF16),
            V((128, 128), BF16),
            V((chunks, subs, WIDE), BF16),
            V((chunks, 4, subs, WIDE), BF16),
            V((subs, 128), BF16),
            V((4, subs, 128), BF16),
            V((4 * slots, CHUNK), BF16),
            V((experts, 2, 4 * slots, units), F32),
            V((experts, 4 * slots, units), BF16),
            V((4 * slots, 128), F32),
            V((chunks, 4, slots, CHUNK), BF16),
            V((chunks, slots // 2, CHUNK), BF16),
            V((chunks, slots // 2, CHUNK), BF16),
            V((chunks, slots, CHUNK), BF16),
            V((chunks, slots, CHUNK), BF16),
            V((chunks, subs, WIDE), BF16),
            V((chunks, subs, WIDE), BF16),
            V((chunks, rows, CHUNK), BF16),
            pltpu.SemaphoreType.DMA((20, chunks + 1)),
            pltpu.SemaphoreType.DMA((5, chunks)),
        ],
        compiler_params=pltpu.CompilerParams(
            collective_id=0, has_side_effects=True, vmem_limit_bytes=64000000
        ),
    )(tokens, expert_ids, route_weight.astype(F32), w_gate, w_up, w_down)


def solution(mesh):
    placed = (
        P(("node", "torus"), None),
        P(("node", "torus"), None),
        P(("node", "torus"), None),
        P("torus", None, "node"),
        P("torus", None, "node"),
        P("torus", "node", None),
    )
    return jax.shard_map(
        shards, mesh=mesh, in_specs=placed, out_specs=P(("node", "torus"), None), check_vma=False
    )
```

time: 158 us -> 74.6 us (0.47)
  blocking collectives: 86 us -> 0 us
  Pallas kernels: 0 us -> 68.7 us
  matrix products: 23.1 us -> 0 us
  between operations: 13.6 us -> 0.01 us
  other arithmetic: 10.1 us -> 0 us
  waiting for transfers between devices: 6.97 us -> 0 us
  starting transfers between devices: 6.65 us -> 0 us
  local copies, waits for them, and re-layouts: 10.9 us -> 5.66 us
    all_to_all x2 -> x0, blocking collectives: 69 us -> none  [the longest x1 48.9 us: shards(): lax.all_to_all(partial_value.astype(jnp.bfloat16), ('node', 'torus'), spl...]
    pallas_call x0 -> x1, Pallas kernels: none -> 68.7 us  [shards(): pl.pallas_call(functools.partial(kernel, groups, chunks, LAGS), out_shape...]
    dot_general x8 -> x0, matrix products: 23.1 us -> none  [the longest x2 14 us: shards(): result = jnp.dot(hidden, w_down[expert], preferred_element_type=jnp.float32)]
    all_gather x2 -> x0, blocking collectives: 16.9 us -> none  [the longest x1 8.75 us: shards(): lax.all_gather(lax.all_to_all(send_scale, 'torus', split_axis=0, concat_a...]
    all_to_all x2 -> x0, starting transfers between devices: 6.65 us -> none  [the longest x1 3.33 us: shards(): lax.all_to_all(send_scale, 'torus', split_axis=0, concat_axis=0, tiled=True)]
    convert_element_type x6 -> x1, local copies, waits for them, and re-layouts: 7.13 us -> 1.4 us  [shards(): route_weight.astype(F32)]
    convert_element_type x6 -> x0, other arithmetic: 4.94 us -> none  [the longest x1 2.61 us: restore(): return blocks.astype(jnp.bfloat16).reshape(count, -1)]
    all_to_all x2 -> x0, waiting for transfers between devices: 4.78 us -> none  [the longest x1 4.78 us: shards(): lax.all_to_all(send_weights, 'torus', split_axis=0, concat_axis=0, tiled=...]
  transfers between devices with their start and end apart: 3 -> 0, of which waited for: 2 -> 0; matrix products, arithmetic and copies ran while one was open for 1% -> 0% of each run, Pallas kernels for 0% -> 0%
where the time goes in v1:
time: 74.6 us; the launch traced here: 74.3 us
  Pallas kernels  68.7 us (92%)
  local copies, waits for them, and re-layouts  5.66 us (8%)
    pallas_call x1, Pallas kernels, shards(): pl.pallas_call(functools.partial(kernel, groups, chunks, LAGS), out_shape...  68.7 us
    unnamed x2, local copies, waits for them, and re-layouts  4.26 us

profile of v1, /device:TPU:0, one launch (start us, length us, event | category | flops | bytes accessed | tf_op | source)
XLA Modules:
  0.0 74.3 jit_solution(14526022973040661144)
XLA Ops:
  0.0 1.4 %copy.9.ids_ref = s32[128,8]{1,0:T(8,128)} copy(s32[128,8]{0,1:T(8,128)} %param.7) | data formatting | bytes 8192 | tf_op args[1]
  1.4 1.4 %copy.10.rw_ref = f32[128,8]{1,0:T(8,128)} copy(bf16[128,8]{0,1:T(8,128)(2,1)} %param.8) | data formatting | bytes 6144 | tf_op jit(solution)/shard_map/convert_element_type | solution.py:343
  2.8 68.7 %shard_map.64 = bf16[128,7168]{1,0:T(8,128)(2,1)} custom-call(bf16[128,7168]{1,0:T(8,128)(2,1)} %tok_hbm.1, s32[128,8]{1,0:T(8,128)} %copy.9.ids_ref, f32[128,8]{1,0:T(8,128)} %copy.10.rw_ref, bf16[2,7168,256]{2,1,0:T(8,128)(2,1)} %wg_hbm.1, bf16[2,7168,256]{2,1,0:T(8,128)(2,1)} %wu_hbm.1, bf16[2,256,7168]{2,1,0:T(8,128)(2,1)} %wd_hbm.1), custom_call_target="tpu_custom_call" | custom-call | tf_op jit(solution)/shard_map/pallas_call | solution.py:307
  71.5 2.8 %copy.12 = bf16[128,7168]{1,0:T(8,128)(2,1)} copy(bf16[128,7168]{1,0:T(8,128)(2,1)} %shard_map.64) | data formatting | bytes 3670016

commit v2 on v1

--- a/solution.py
+++ b/solution.py
@@ -73,35 +73,34 @@
     for peer in at_z[1:] + [at_x, at_y]:
         pl.semaphore_signal(barrier, inc=1, device_id=peer, device_id_type=MESH)
 
-    col = lax.broadcasted_iota(jnp.int32, (rows, subs), 1)
-    gid = jnp.bitwise_xor(col // SUB, jnp.full((rows, subs), torus, jnp.int32))
-    slot_of = (col // PARTS) % CAP
-    part_of = col % PARTS
-    hit = jnp.zeros((rows, subs), F32)
-    chosen = [jnp.zeros((rows, subs), F32) for _ in range(experts)]
-    for k in range(ids_ref.shape[1]):
-        named = jnp.broadcast_to(ids_ref[:, k : k + 1], (rows, subs))
-        weight = jnp.broadcast_to(rw_ref[:, k : k + 1], (rows, subs))
+    row = lax.broadcasted_iota(jnp.int32, (subs, rows), 0)
+    gid = jnp.bitwise_xor(row // SUB, jnp.full((subs, rows), torus, jnp.int32))
+    slot_of = (row // PARTS) % CAP
+    part_of = row % PARTS
+    hit = jnp.zeros((subs, rows), F32)
+    chosen = [jnp.zeros((subs, rows), F32) for _ in range(experts)]
+    weights = rw_ref[...].astype(F32)
+    for k in range(ids_ref.shape[0]):
+        named = jnp.broadcast_to(ids_ref[k : k + 1, :], (subs, rows))
+        weight = jnp.broadcast_to(weights[k : k + 1, :], (subs, rows))
         for e in range(experts):
             same = named == gid * experts + e
             hit = jnp.where(same, 1.0, hit)
             chosen[e] = jnp.where(same, weight, chosen[e])
-    lower = lax.broadcasted_iota(jnp.int32, (rows, rows), 1) < lax.broadcasted_iota(
-        jnp.int32, (rows, rows), 0
+    lower = lax.broadcasted_iota(jnp.int32, (rows, rows), 0) < lax.broadcasted_iota(
+        jnp.int32, (rows, rows), 1
     )
-    before = dot(lower.astype(F32).astype(BF16), hit.astype(BF16))
+    before = dot(hit.astype(BF16), lower.astype(F32).astype(BF16))
     onehot = jnp.where(before == slot_of.astype(F32), hit, 0.0)
-    for q in range(PARTS):
-        mine = jnp.where(part_of == q, onehot, 0.0)
-        place_t[q] = mine.astype(BF16)
-        place[q] = mine.T.astype(BF16)
     lane = lax.broadcasted_iota(jnp.int32, (subs, 128), 1)
     wrow = jnp.zeros((subs, 128), F32)
     for e in range(experts):
-        total = jnp.sum((onehot * chosen[e]).T, axis=1, keepdims=True)
+        total = jnp.sum(onehot * chosen[e], axis=1, keepdims=True)
         wrow = jnp.where(lane == e, total, wrow)
     wsent[...] = wrow.astype(BF16)
     wheld[0, 0:SUB] = wrow[0:SUB].astype(BF16)
+    for q in range(PARTS):
+        place[q] = jnp.where(part_of == q, onehot, 0.0).astype(BF16)
     pr = lax.broadcasted_iota(jnp.int32, (128, 128), 0)
     pc = lax.broadcasted_iota(jnp.int32, (128, 128), 1)
     ur = 128 // PARTS
@@ -186,10 +185,14 @@
 
     exchange(chunks)
     l2, l3, l4 = lags
+    flip_at = min(chunks, l4) - 1
     for step in range(chunks + l4):
         if step < chunks:
             make(step)
             exchange(step)
+        if step == flip_at:
+            for q in range(PARTS):
+                place_t[q] = place[q].astype(F32).T.astype(BF16)
         if step == l2:
             spread(chunks)
         if 0 <= step - l2 < chunks:
@@ -291,7 +294,7 @@
         out_cp[k].wait()
 
 
-LAGS = (1, 2, 3)
+LAGS = (3, 6, 9)
 
 
 def shards(tokens, expert_ids, route_weight, w_gate, w_up, w_down):
@@ -340,7 +343,7 @@
         compiler_params=pltpu.CompilerParams(
             collective_id=0, has_side_effects=True, vmem_limit_bytes=64000000
         ),
-    )(tokens, expert_ids, route_weight.astype(F32), w_gate, w_up, w_down)
+    )(tokens, expert_ids.T, route_weight.T, w_gate, w_up, w_down)
 
 
 def solution(mesh):

time: 74.6 us -> 57.6 us (0.77)
  Pallas kernels: 68.7 us -> 54.5 us
  local copies, waits for them, and re-layouts: 5.66 us -> 2.85 us
    pallas_call x1, Pallas kernels: 68.7 us -> 54.5 us  [shards(): pl.pallas_call(functools.partial(kernel, groups, chunks, LAGS), out_shape...]
    unnamed x2 -> x1, local copies, waits for them, and re-layouts: 4.26 us -> 2.85 us
    convert_element_type x1 -> x0, local copies, waits for them, and re-layouts: 1.4 us -> none  [shards(): route_weight.astype(F32)]
where the time goes in v2:
time: 57.6 us; the launch traced here: 57.4 us
  Pallas kernels  54.5 us (95%)
  local copies, waits for them, and re-layouts  2.85 us (5%)
    pallas_call x1, Pallas kernels, shards(): pl.pallas_call(functools.partial(kernel, groups, chunks, LAGS), out_shape...  54.5 us
    unnamed x1, local copies, waits for them, and re-layouts  2.85 us

profile of v2, /device:TPU:0, one launch (start us, length us, event | category | flops | bytes accessed | tf_op | source)
XLA Modules:
  0.0 57.4 jit_solution(9811306025872023418)
XLA Ops:
  0.0 54.5 %shard_map.64 = bf16[128,7168]{1,0:T(8,128)(2,1)} custom-call(bf16[128,7168]{1,0:T(8,128)(2,1)} %tok_hbm.1, s32[8,128]{1,0:T(8,128)} %bitcast.2, bf16[8,128]{1,0:T(8,128)(2,1)} %bitcast.3, bf16[2,7168,256]{2,1,0:T(8,128)(2,1)} %wg_hbm.1, bf16[2,7168,256]{2,1,0:T(8,128)(2,1)} %wu_hbm.1, bf16[2,256,7168]{2,1,0:T(8,128)(2,1)} %wd_hbm.1), custom_call_target="tpu_custom_call" | custom-call | tf_op jit(solution)/shard_map/pallas_call | solution.py:310
  54.5 2.8 %copy.8 = bf16[128,7168]{1,0:T(8,128)(2,1)} copy(bf16[128,7168]{1,0:T(8,128)(2,1)} %shard_map.64) | data formatting | bytes 3670016
